TPU v7x, 32 devices: a whole 2x2x4 slice. The times are simulated.
32 devices in a mesh: cache: 4 (over x, core), expert: 8 (over z, y).
Axes of the slice: x: 2, y: 2, z: 4, core: 2. Of those that a mesh axis runs over, the one named last changes fastest.
Arguments:
- queries: bfloat16 [2, 32, 2048], P(None, 'expert'), may hold values from -16 to 16
- k_cache: bfloat16 [32, 4096, 256], P('expert', 'cache'), may hold values from -6 to 6
- v_cache: bfloat16 [32, 4096, 256], P('expert', 'cache'), may hold values from -6 to 6
- lengths: int32 [32], P('expert'), may hold values from 1 to 4094
- w_out: bfloat16 [2048, 2880], P('cache'), may hold values from -0.125 to 0.125
- norm_gain: float32 [2880], replicated, may hold values from 0.25 to 1.75
- w_gate: bfloat16 [8, 2880, 1440], P('cache', 'expert'), may hold values from -0.109375 to 0.109375
- w_up: bfloat16 [8, 2880, 1440], P('cache', 'expert'), may hold values from -0.109375 to 0.109375
- w_down: bfloat16 [8, 1440, 2880], P('cache', None, 'expert'), may hold values from -0.15625 to 0.15625
- expert_ids: int32 [2, 32, 4], P(None, 'expert'), may hold values from 0 to 7, all different within a row; in each aligned block of 4 rows (0 to 3, 4 to 7, ..., all dimensions but the last counted through in order) at most 2 rows name the same one
- gate_weights: float32 [2, 32, 4], P(None, 'expert'), may hold values from 0.1 to 1
Outputs:
- mixed: bfloat16 [2, 32, 2880], P(None, 'expert')
- gate_owner: bfloat16 [8, 2880, 1440], P('expert', None, 'cache')
- up_owner: bfloat16 [8, 2880, 1440], P('expert', None, 'cache')
- down_owner: bfloat16 [8, 1440, 2880], P('expert', 'cache')
Inputs may be any that keep to these rules, and one draw needn't show every extreme that they name: `expert_ids`: in each step the 4 rows of one index of expert name one expert at most 2 times; a row names 4 different experts.
All inputs are finite; a program needn't handle non-finite values.
Results may differ from a plain program's by a relative error of at most 0.015.
Values may be sent and summed in bfloat16 or wider, within the bound.
A program may use at most 64 MiB of HBM per device.

v0:
```python
import math
import jax
import jax.numpy as jnp
from jax import lax
from jax.sharding import PartitionSpec as P

D = 2880
QH = 32
KVH = 4
HD = 64
TOP = 4


def joined(part, axis, combine):
    gathered = jax.tree.map(lambda a: lax.all_gather(a, axis), part)

    def take(source):
        return jax.tree.map(lambda a: lax.dynamic_index_in_dim(a, source, 0, False), gathered)

    return lax.fori_loop(
        1, lax.axis_size(axis), lambda source, state: combine(state, take(source)), take(0)
    )


def merge_partials(first, second):
    first_high, first_mass, first_accum = first
    second_high, second_mass, second_accum = second
    shared = jnp.maximum(first_high, second_high)
    first_factor = jnp.exp(first_high - shared)
    second_factor = jnp.exp(second_high - shared)
    head_width = first_accum.shape[-1] // first_high.shape[-1]
    accum = first_accum * jnp.repeat(first_factor, head_width, axis=-1) + second_accum * jnp.repeat(
        second_factor, head_width, axis=-1
    )
    return (shared, first_mass * first_factor + second_mass * second_factor, accum)


def shards(
    queries,
    k_cache,
    v_cache,
    lengths,
    w_out,
    norm_gain,
    w_gate,
    w_up,
    w_down,
    expert_ids,
    gate_weights,
):
    gate_owner, up_owner = (
        lax.all_to_all(
            lax.all_to_all(w_gate, "cache", split_axis=2, concat_axis=0, tiled=True),
            "expert",
            split_axis=0,
            concat_axis=1,
            tiled=True,
        ),
        lax.all_to_all(
            lax.all_to_all(w_up, "cache", split_axis=2, concat_axis=0, tiled=True),
            "expert",
            split_axis=0,
            concat_axis=1,
            tiled=True,
        ),
    )
    down_owner = lax.all_to_all(
        lax.all_to_all(w_down, "cache", split_axis=1, concat_axis=0, tiled=True),
        "expert",
        split_axis=0,
        concat_axis=2,
        tiled=True,
    )
    cache_count = lax.axis_size("cache")
    cache_place = lax.axis_index("cache")
    step_count = queries.shape[0]
    row_count = k_cache.shape[0]
    positions = k_cache.shape[1]
    group_size = QH // KVH
    query_heads = queries.reshape(step_count, row_count, KVH, group_size, HD)
    key_heads = k_cache.reshape(row_count, positions, KVH, HD)
    value_heads = v_cache.reshape(row_count, positions, KVH, HD)
    scores = jnp.einsum(
        "srhgd,rphd->srhgp", query_heads, key_heads, preferred_element_type=jnp.float32
    ) * (1.0 / math.sqrt(HD))
    position = cache_place * positions + jnp.arange(positions, dtype=jnp.int32)
    limit = lengths[None, :] + jnp.arange(step_count, dtype=jnp.int32)[:, None] + 1
    visible = (position[None, None, :] < limit[:, :, None])[:, :, None, None, :]
    highest = jnp.max(jnp.where(visible, scores, -1e30), axis=-1)
    weights = jnp.where(visible, jnp.exp(scores - highest[..., None]), 0.0)
    mass = jnp.sum(weights, axis=-1).reshape(step_count, row_count, QH)
    accum = jnp.einsum(
        "srhgp,rphd->srhgd",
        weights.astype(jnp.bfloat16),
        value_heads,
        preferred_element_type=jnp.float32,
    )
    accum = accum.reshape(step_count, row_count, QH * HD)
    highest = highest.reshape(step_count, row_count, QH)
    own_width = w_out.shape[0]
    all_high, all_mass, all_accum = joined((highest, mass, accum), "cache", merge_partials)
    heads_out = all_accum / jnp.repeat(all_mass, HD, axis=-1)
    own_out = lax.dynamic_slice_in_dim(heads_out, cache_place * own_width, own_width, 2)
    own_rows = own_out.astype(jnp.bfloat16).reshape(step_count * row_count, own_width)
    projected = jnp.dot(own_rows, w_out, preferred_element_type=jnp.float32)
    attention = lax.psum(projected, "cache")
    scale = lax.rsqrt(jnp.mean(attention * attention, axis=-1, keepdims=True) + 1e-05)
    normed = (attention * scale * norm_gain).astype(jnp.bfloat16).reshape(step_count, row_count, D)
    experts_total = w_gate.shape[0] * cache_count
    capacity = max(2, (row_count * TOP + experts_total - 1) // experts_total)
    expert_range = jnp.arange(experts_total, dtype=jnp.int32)
    onehot = (expert_ids[..., None] == expert_range).astype(jnp.float32)
    chosen = jnp.sum(onehot, axis=2)
    gate_map = jnp.sum(onehot * gate_weights[..., None], axis=2)
    earlier = jnp.tril(jnp.ones((row_count, row_count), jnp.float32), -1)
    ranks = jnp.einsum("rq,sqe->sre", earlier, chosen, precision=lax.Precision.HIGHEST)
    slot_table = (ranks[..., None] == jnp.arange(capacity, dtype=jnp.float32)).astype(
        jnp.float32
    ) * chosen[..., None]
    outgoing = jnp.einsum(
        "srec,srd->escd",
        slot_table.astype(jnp.bfloat16),
        normed,
        preferred_element_type=jnp.float32,
    )
    outgoing = outgoing.astype(jnp.bfloat16).reshape(experts_total, step_count * capacity, D)
    slots = lax.all_to_all(outgoing, "expert", split_axis=0, concat_axis=0, tiled=True)
    source_count = slots.shape[0]
    item_count = slots.shape[1]
    slot_rows = slots.reshape(source_count * item_count, D)
    gate_value = jnp.dot(slot_rows, gate_owner[0], preferred_element_type=jnp.float32)
    up_value = jnp.dot(slot_rows, up_owner[0], preferred_element_type=jnp.float32)
    hidden = (jax.nn.silu(gate_value) * up_value).astype(jnp.bfloat16)
    partial_out = jnp.dot(hidden, down_owner[0], preferred_element_type=jnp.float32).reshape(
        source_count, item_count, D
    )
    expert_out = lax.psum(partial_out, "cache").astype(jnp.bfloat16)
    returned = lax.all_to_all(expert_out, "expert", split_axis=0, concat_axis=0, tiled=True)
    back_width = returned.shape[-1]
    returned = returned.reshape(experts_total, step_count, capacity, back_width)
    combined = jnp.einsum(
        "srec,escd->srd",
        slot_table * gate_map[..., None],
        returned.astype(jnp.float32),
        precision=lax.Precision.HIGHEST,
    )
    attention_rows = attention.reshape(step_count, row_count, D)
    mixed = (attention_rows + combined).astype(jnp.bfloat16)
    return (mixed, gate_owner, up_owner, down_owner)


def solution(mesh):
    return jax.shard_map(
        shards,
        mesh=mesh,
        in_specs=(
            P(None, "expert", None),
            P("expert", "cache", None),
            P("expert", "cache", None),
            P("expert"),
            P("cache", None),
            P(),
            P("cache", "expert", None),
            P("cache", "expert", None),
            P("cache", None, "expert"),
            P(None, "expert", None),
            P(None, "expert", None),
        ),
        out_specs=(
            P(None, "expert", None),
            P("expert", None, "cache"),
            P("expert", None, "cache"),
            P("expert", "cache", None),
        ),
        check_vma=False,
    )
```

profile of v0, /device:TPU:0, one launch (start us, length us, event | category | flops | bytes accessed | tf_op | source)
XLA Modules:
  0.0 412.6 jit_solution(15657608075601051097)
XLA Ops:
  7.2 0.9 add_add_fusion
  9.0 4.0 copy.74
  13.0 2.1 select_reduce_fusion
  15.1 0.9 copy-done.2
  16.5 6.7 %all_gather.10 = f32[4,2,4,32]{3,2,1,0:T(4,128)} all-gather(f32[1,2,4,32]{3,2,1,0:T(4,128)S(1)} %all_gather_reshape.10), channel_id=1, replica_groups=mesh['cache'=4,'expert'=8] {'cache'}, dimensions={0}, use_global_device_ids=true | all-gather | bytes 5120 | tf_op jit(solution)/shard_map/all_gather | solution.py:15
  24.0 5.8 %all_gather.9 = f32[4,2,4,32]{3,2,1,0:T(4,128)} all-gather(f32[1,2,4,32]{3,2,1,0:T(4,128)S(1)} %all_gather_reshape.9), channel_id=1, replica_groups=mesh['cache'=4,'expert'=8] {'cache'}, dimensions={0}, use_global_device_ids=true | all-gather | bytes 5120 | tf_op jit(solution)/shard_map/all_gather | solution.py:15
  30.5 3.9 copy.78
  34.4 2.6 convolution_bitcast_fusion.1
  37.2 6.0 %all_gather.11 = f32[4,2,4,2048]{3,2,1,0:T(4,128)S(1)} all-gather(f32[1,2,4,2048]{3,2,1,0:T(4,128)S(1)} %all_gather_reshape.11), channel_id=1, replica_groups=mesh['cache'=4,'expert'=8] {'cache'}, dimensions={0}, use_global_device_ids=true | all-gather | bytes 327680 | tf_op jit(solution)/shard_map/all_gather | solution.py:15
  43.2 3.6 while.19
  47.0 1.5 fusion.36
  48.9 32.8 %all-reduce.3.cloned.1.call-done = f32[8,2880]{1,0:T(8,128)} async-done(((f32[8,2880]{1,0:T(8,128)}), f32[8,2880]{1,0:T(8,128)}) %all-reduce.3.cloned.1.call-update) | async-done | bytes 92176 | tf_op jit(solution)/shard_map/psum | solution.py:106
  81.7 1.0 multiply_reduce_fusion
  82.8 1.0 multiply_convert_fusion
  84.8 5.5 %all-to-all-start = ((bf16[8,4,2880]{2,1,0:T(4,128)(2,1)}), bf16[8,4,2880]{2,1,0:T(4,128)(2,1)S(1)}, u32[]{:S(2)}, u32[]{:S(2)}) async-start(bf16[8,4,2880]{2,1,0:T(4,128)(2,1)} %copy.80), calls=%async_computation | async-start | bytes 376832 | tf_op jit(solution)/shard_map/all_to_all | solution.py:127
  90.3 6.8 %copy.81 = bf16[2,360,1440]{1,0,2:T(2,128)(2,1)} copy(bf16[2,360,1440]{2,1,0:T(8,128)(2,1)} %param.19) | data formatting | bytes 4147200 | tf_op args[6]
  97.1 0.9 all-to-all-done
  98.0 4.5 %all-to-all-start.1 = ((bf16[2,360,1440]{1,0,2:T(2,128)(2,1)}), bf16[2,360,1440]{1,0,2:T(2,128)(2,1)}, u32[]{:S(2)}, u32[]{:S(2)}) async-start(bf16[2,360,1440]{1,0,2:T(2,128)(2,1)} %copy.81), calls=%async_computation.1 | async-start | bytes 4423680 | tf_op jit(solution)/shard_map/all_to_all | solution.py:53
  102.5 6.8 %copy.84 = bf16[2,360,1440]{1,0,2:T(2,128)(2,1)} copy(bf16[2,360,1440]{2,1,0:T(8,128)(2,1)} %param.20) | data formatting | bytes 4147200 | tf_op args[7]
  109.3 20.2 %all-to-all-done.1 = bf16[2,360,1440]{1,0,2:T(2,128)(2,1)} async-done(((bf16[2,360,1440]{1,0,2:T(2,128)(2,1)}), bf16[2,360,1440]{1,0,2:T(2,128)(2,1)}, u32[]{:S(2)}, u32[]{:S(2)}) %all-to-all-start.1) | async-done | bytes 2073632 | tf_op jit(solution)/shard_map/all_to_all | solution.py:53
  129.5 4.5 %all-to-all-start.3 = ((bf16[2,360,1440]{1,0,2:T(2,128)(2,1)}), bf16[2,360,1440]{1,0,2:T(2,128)(2,1)}, u32[]{:S(2)}, u32[]{:S(2)}) async-start(bf16[2,360,1440]{1,0,2:T(2,128)(2,1)} %copy.84), calls=%async_computation.3 | async-start | bytes 4423680 | tf_op jit(solution)/shard_map/all_to_all | solution.py:60
  134.0 12.9 %copy.87 = bf16[2,1440,360]{2,0,1:T(2,128)(2,1)} copy(bf16[2,1440,360]{2,1,0:T(8,128)(2,1)} %param.21) | data formatting | bytes 4147200 | tf_op args[8]
  146.9 14.0 %all-to-all-done.3 = bf16[2,360,1440]{1,0,2:T(2,128)(2,1)} async-done(((bf16[2,360,1440]{1,0,2:T(2,128)(2,1)}), bf16[2,360,1440]{1,0,2:T(2,128)(2,1)}, u32[]{:S(2)}, u32[]{:S(2)}) %all-to-all-start.3) | async-done | bytes 2073632 | tf_op jit(solution)/shard_map/all_to_all | solution.py:60
  160.9 4.5 %all-to-all-start.5 = ((bf16[2,1440,360]{2,0,1:T(2,128)(2,1)}), bf16[2,1440,360]{2,0,1:T(2,128)(2,1)}, u32[]{:S(2)}, u32[]{:S(2)}) async-start(bf16[2,1440,360]{2,0,1:T(2,128)(2,1)} %copy.87), calls=%async_computation.5 | async-start | bytes 4423680 | tf_op jit(solution)/shard_map/all_to_all | solution.py:68
  165.4 3.3 copy.82
  168.7 23.6 %all-to-all-done.5 = bf16[2,1440,360]{2,0,1:T(2,128)(2,1)} async-done(((bf16[2,1440,360]{2,0,1:T(2,128)(2,1)}), bf16[2,1440,360]{2,0,1:T(2,128)(2,1)}, u32[]{:S(2)}, u32[]{:S(2)}) %all-to-all-start.5) | async-done | bytes 2073632 | tf_op jit(solution)/shard_map/all_to_all | solution.py:68
  192.3 5.1 %all-to-all-start.2 = ((bf16[8,360,360]{1,2,0:T(8,128)(2,1)}), bf16[8,360,360]{1,2,0:T(8,128)(2,1)}, u32[]{:S(2)}, u32[]{:S(2)}) async-start(bf16[8,360,360]{1,2,0:T(8,128)(2,1)} %bitcast.104), calls=%async_computation.2 | async-start | bytes 4423680 | tf_op jit(solution)/shard_map/all_to_all | solution.py:52
  197.4 3.4 copy.85
  200.8 47.1 %all-to-all-done.2 = bf16[8,360,360]{1,2,0:T(8,128)(2,1)} async-done(((bf16[8,360,360]{1,2,0:T(8,128)(2,1)}), bf16[8,360,360]{1,2,0:T(8,128)(2,1)}, u32[]{:S(2)}, u32[]{:S(2)}) %all-to-all-start.2) | async-done | bytes 2073632 | tf_op jit(solution)/shard_map/all_to_all | solution.py:52
  247.9 4.4 %all-to-all-start.4 = ((bf16[8,360,360]{1,2,0:T(8,128)(2,1)}), bf16[8,360,360]{1,2,0:T(8,128)(2,1)}, u32[]{:S(2)}, u32[]{:S(2)}) async-start(bf16[8,360,360]{1,2,0:T(8,128)(2,1)} %bitcast.105), calls=%async_computation.4 | async-start | bytes 4423680 | tf_op jit(solution)/shard_map/all_to_all | solution.py:59
  252.3 3.3 copy.88
  255.6 46.9 %all-to-all-done.4 = bf16[8,360,360]{1,2,0:T(8,128)(2,1)} async-done(((bf16[8,360,360]{1,2,0:T(8,128)(2,1)}), bf16[8,360,360]{1,2,0:T(8,128)(2,1)}, u32[]{:S(2)}, u32[]{:S(2)}) %all-to-all-start.4) | async-done | bytes 2073632 | tf_op jit(solution)/shard_map/all_to_all | solution.py:59
  302.6 4.5 %all-to-all-start.6 = ((bf16[8,360,360]{2,1,0:T(8,128)(2,1)}), bf16[8,360,360]{2,1,0:T(8,128)(2,1)}, u32[]{:S(2)}, u32[]{:S(2)}) async-start(bf16[8,360,360]{2,1,0:T(8,128)(2,1)} %bitcast.103), calls=%async_computation.6 | async-start | bytes 4423680 | tf_op jit(solution)/shard_map/all_to_all | solution.py:67
  307.2 4.2 %copy.83 = bf16[8,360,360]{2,1,0:T(8,128)(2,1)} copy(bf16[8,360,360]{1,2,0:T(8,128)(2,1)} %all-to-all-done.2) | data formatting | bytes 4147200 | tf_op jit(solution)/shard_map/all_to_all | solution.py:52
  311.4 4.2 %copy.86 = bf16[8,360,360]{2,1,0:T(8,128)(2,1)} copy(bf16[8,360,360]{1,2,0:T(8,128)(2,1)} %all-to-all-done.4) | data formatting | bytes 4147200 | tf_op jit(solution)/shard_map/all_to_all | solution.py:59
  315.6 2.2 fusion.37
  318.4 38.9 %all-to-all-done.6 = bf16[8,360,360]{2,1,0:T(8,128)(2,1)} async-done(((bf16[8,360,360]{2,1,0:T(8,128)(2,1)}), bf16[8,360,360]{2,1,0:T(8,128)(2,1)}, u32[]{:S(2)}, u32[]{:S(2)}) %all-to-all-start.6) | async-done | bytes 2073632 | tf_op jit(solution)/shard_map/all_to_all | solution.py:67
  357.3 3.3 copy.89
  360.6 4.8 %reshape.124 = bf16[360,2880,1]{1,0,2:T(8,128)(2,1)} reshape(bf16[1,360,8,360]{3,2,1,0:T(8,128)(2,1)} %copy.89) | data formatting | bytes 4147200 | tf_op jit(solution)/shard_map/squeeze | solution.py:134
  365.4 2.0 fusion.15
  367.5 14.8 %all-reduce.4 = bf16[8,4,2880]{2,0,1:T(8,128)(2,1)} all-reduce(f32[8,4,2880]{2,0,1:T(8,128)S(1)} %fusion.15), channel_id=1, replica_groups=mesh['cache'=4,'expert'=8] {'cache'}, use_global_device_ids=true, to_apply=%region_8.9 | all-reduce | flops 92160 | bytes 552960 | tf_op jit(solution)/shard_map/psum | solution.py:137
  382.2 1.7 copy.91
  383.9 4.3 %all-to-all-start.7 = ((bf16[8,4,2880]{2,1,0:T(4,128)(2,1)}), bf16[8,4,2880]{2,1,0:T(4,128)(2,1)S(1)}, u32[]{:S(2)}, u32[]{:S(2)}) async-start(bf16[8,4,2880]{2,1,0:T(4,128)(2,1)} %copy.91), calls=%async_computation.7 | async-start | bytes 376832 | tf_op jit(solution)/shard_map/all_to_all | solution.py:138
  388.3 4.2 %copy.95 = bf16[1,360,8,360]{1,3,2,0:T(8,128)(2,1)} copy(bf16[1,360,8,360]{3,1,2,0:T(8,128)(2,1)} %bitcast.31) | data formatting | bytes 4147200 | tf_op jit(solution)/shard_map/all_to_all | solution.py:67
  392.5 4.1 %copy.96 = bf16[1,2880,360]{1,2,0:T(8,128)(2,1)} copy(bf16[1,2880,360]{2,1,0:T(8,128)(2,1)} %bitcast.100) | data formatting | bytes 4147200
  396.6 4.1 %copy.97 = bf16[1,2880,360]{1,2,0:T(8,128)(2,1)} copy(bf16[1,2880,360]{2,1,0:T(8,128)(2,1)} %bitcast.101) | data formatting | bytes 4147200
  400.7 4.1 %copy.98 = bf16[1,360,2880]{2,1,0:T(8,128)(2,1)} copy(bf16[1,360,2880]{1,2,0:T(8,128)(2,1)} %bitcast.106) | data formatting | bytes 4147200
  404.9 0.9 fusion.4
  (63 shorter events, 8.8 us)
Async XLA Ops:
  7.2 39.9 %copy-start = (bf16[512,2880]{0,1:T(8,128)(2,1)S(1)}, bf16[512,2880]{0,1:T(8,128)(2,1)}, u32[]{:S(2)}) copy-start(bf16[512,2880]{0,1:T(8,128)(2,1)} %param.17) | copy-start | bytes 8847364
  7.2 74.6 %all-reduce.3.cloned.1.call-start = ((), (), s32[]{:S(2)}) async-start(), calls=%async_computation.8 | async-start | bytes 188416 | tf_op jit(solution)/shard_map/psum | solution.py:106
  15.1 1.0 copy-start.2
  46.7 1.8 copy-start.5
  46.7 1.8 copy-start.6
  46.8 36.0 %copy-start.4 = (f32[2880]{0:T(1024)S(1)}, f32[2880]{0:T(1024)}, u32[]{:S(2)}) copy-start(f32[2880]{0:T(1024)} %param.18) | copy-start | bytes 34564
  84.8 13.2 %all-to-all-start = ((bf16[8,4,2880]{2,1,0:T(4,128)(2,1)}), bf16[8,4,2880]{2,1,0:T(4,128)(2,1)S(1)}, u32[]{:S(2)}, u32[]{:S(2)}) async-start(bf16[8,4,2880]{2,1,0:T(4,128)(2,1)} %copy.80), calls=%async_computation | async-start | bytes 376832 | tf_op jit(solution)/shard_map/all_to_all | solution.py:127
  98.0 31.4 %all-to-all-start.1 = ((bf16[2,360,1440]{1,0,2:T(2,128)(2,1)}), bf16[2,360,1440]{1,0,2:T(2,128)(2,1)}, u32[]{:S(2)}, u32[]{:S(2)}) async-start(bf16[2,360,1440]{1,0,2:T(2,128)(2,1)} %copy.81), calls=%async_computation.1 | async-start | bytes 4423680 | tf_op jit(solution)/shard_map/all_to_all | solution.py:53
  129.5 31.4 %all-to-all-start.3 = ((bf16[2,360,1440]{1,0,2:T(2,128)(2,1)}), bf16[2,360,1440]{1,0,2:T(2,128)(2,1)}, u32[]{:S(2)}, u32[]{:S(2)}) async-start(bf16[2,360,1440]{1,0,2:T(2,128)(2,1)} %copy.84), calls=%async_computation.3 | async-start | bytes 4423680 | tf_op jit(solution)/shard_map/all_to_all | solution.py:60
  160.9 31.4 %all-to-all-start.5 = ((bf16[2,1440,360]{2,0,1:T(2,128)(2,1)}), bf16[2,1440,360]{2,0,1:T(2,128)(2,1)}, u32[]{:S(2)}, u32[]{:S(2)}) async-start(bf16[2,1440,360]{2,0,1:T(2,128)(2,1)} %copy.87), calls=%async_computation.5 | async-start | bytes 4423680 | tf_op jit(solution)/shard_map/all_to_all | solution.py:68
  192.3 55.6 %all-to-all-start.2 = ((bf16[8,360,360]{1,2,0:T(8,128)(2,1)}), bf16[8,360,360]{1,2,0:T(8,128)(2,1)}, u32[]{:S(2)}, u32[]{:S(2)}) async-start(bf16[8,360,360]{1,2,0:T(8,128)(2,1)} %bitcast.104), calls=%async_computation.2 | async-start | bytes 4423680 | tf_op jit(solution)/shard_map/all_to_all | solution.py:52
  247.9 54.6 %all-to-all-start.4 = ((bf16[8,360,360]{1,2,0:T(8,128)(2,1)}), bf16[8,360,360]{1,2,0:T(8,128)(2,1)}, u32[]{:S(2)}, u32[]{:S(2)}) async-start(bf16[8,360,360]{1,2,0:T(8,128)(2,1)} %bitcast.105), calls=%async_computation.4 | async-start | bytes 4423680 | tf_op jit(solution)/shard_map/all_to_all | solution.py:59
  302.6 54.7 %all-to-all-start.6 = ((bf16[8,360,360]{2,1,0:T(8,128)(2,1)}), bf16[8,360,360]{2,1,0:T(8,128)(2,1)}, u32[]{:S(2)}, u32[]{:S(2)}) async-start(bf16[8,360,360]{2,1,0:T(8,128)(2,1)} %bitcast.103), calls=%async_computation.6 | async-start | bytes 4423680 | tf_op jit(solution)/shard_map/all_to_all | solution.py:67
  315.6 2.3 copy-start.1
  365.4 22.8 %copy-start.3 = (f32[8,2880]{1,0:T(8,128)S(1)}, f32[8,2880]{1,0:T(8,128)}, u32[]{:S(2)}) copy-start(f32[8,2880]{1,0:T(8,128)} %all-reduce.3.cloned.1.call-done) | copy-start | bytes 276484
  383.9 20.9 %all-to-all-start.7 = ((bf16[8,4,2880]{2,1,0:T(4,128)(2,1)}), bf16[8,4,2880]{2,1,0:T(4,128)(2,1)S(1)}, u32[]{:S(2)}, u32[]{:S(2)}) async-start(bf16[8,4,2880]{2,1,0:T(4,128)(2,1)} %copy.91), calls=%async_computation.7 | async-start | bytes 376832 | tf_op jit(solution)/shard_map/all_to_all | solution.py:138
Sparse Core Ops, SparseCore 0:
  48.7 33.0 all-reduce.2
where the time goes:
time: 415 us; the launch traced here: 413 us
  waiting for transfers between devices  225 us (54%)
  local copies, waits for them, and re-layouts  85.2 us (21%)
  starting transfers between devices  37.3 us (9%)
  blocking collectives  33.2 us (8%)
  between operations  14.3 us (3%)
  matrix products  12.3 us (3%)
  other arithmetic  5.74 us (1%)
    unnamed x22, local copies, waits for them, and re-layouts  47.8 us
    all_to_all x1, waiting for transfers between devices, shards(): lax.all_to_all(lax.all_to_all(w_gate, 'cache', split_axis=2, concat_axis=...  47.1 us
    all_to_all x1, waiting for transfers between devices, shards(): lax.all_to_all(lax.all_to_all(w_up, 'cache', split_axis=2, concat_axis=0,...  46.9 us
    all_to_all x1, waiting for transfers between devices, shards(): lax.all_to_all(lax.all_to_all(w_down, 'cache', split_axis=1, concat_axis=...  38.9 us
    psum x1, waiting for transfers between devices, shards(): attention = lax.psum(projected, 'cache')  32.8 us
    all_to_all x1, waiting for transfers between devices, shards(): lax.all_to_all(w_down, 'cache', split_axis=1, concat_axis=0, tiled=True)  23.6 us
    all_to_all x1, waiting for transfers between devices, shards(): lax.all_to_all(w_gate, 'cache', split_axis=2, concat_axis=0, tiled=True)  20.2 us
    all_gather x3, blocking collectives, joined(): gathered = jax.tree.map(lambda a: lax.all_gather(a, axis), part)  18.5 us
  transfers between devices with their start and end apart: 9, of which 8 were waited for; matrix products, arithmetic and copies ran while one was open for 16% of the time, Pallas kernels for 0%

commit v1 on v0

--- a/solution.py
+++ b/solution.py
@@ -9,6 +9,11 @@
 KVH = 4
 HD = 64
 TOP = 4
+
+
+def place_joints(local_array):
+    d_next = lax.all_gather(local_array, axis_name="cache")
+    return jnp.sum(d_next, axis=0)
 
 
 def joined(part, axis, combine):
@@ -103,7 +108,7 @@
     own_out = lax.dynamic_slice_in_dim(heads_out, cache_place * own_width, own_width, 2)
     own_rows = own_out.astype(jnp.bfloat16).reshape(step_count * row_count, own_width)
     projected = jnp.dot(own_rows, w_out, preferred_element_type=jnp.float32)
-    attention = lax.psum(projected, "cache")
+    attention = place_joints(projected)
     scale = lax.rsqrt(jnp.mean(attention * attention, axis=-1, keepdims=True) + 1e-05)
     normed = (attention * scale * norm_gain).astype(jnp.bfloat16).reshape(step_count, row_count, D)
     experts_total = w_gate.shape[0] * cache_count

time: 415 us -> 369 us (0.89)
  waiting for transfers between devices: 225 us -> 195 us
  between operations: 14.3 us -> 0.9 us
  blocking collectives: 33.2 us -> 39.3 us
  starting transfers between devices: 37.3 us -> 32.9 us
    psum x1 -> x0, waiting for transfers between devices: 32.8 us -> none  [shards(): attention = lax.psum(projected, 'cache')]
    all_gather x0 -> x1, blocking collectives: none -> 6.62 us  [place_joints(): d_next = lax.all_gather(local_array, axis_name='cache')]
    unnamed x22 -> x34, local copies, waits for them, and re-layouts: 47.8 us -> 49.9 us
  transfers between devices with their start and end apart: 9 -> 8, of which waited for: 8 -> 7; matrix products, arithmetic and copies ran while one was open for 16% -> 16% of each run, Pallas kernels for 0% -> 0%
where the time goes in v1:
time: 369 us; the launch traced here: 367 us
  waiting for transfers between devices  195 us (53%)
  local copies, waits for them, and re-layouts  83 us (22%)
  blocking collectives  39.3 us (11%)
  starting transfers between devices  32.9 us (9%)
  matrix products  11.6 us (3%)
  other arithmetic  3.89 us (1%)
    unnamed x34, local copies, waits for them, and re-layouts  49.9 us
    all_to_all x1, waiting for transfers between devices, shards(): lax.all_to_all(lax.all_to_all(w_gate, 'cache', split_axis=2, concat_axis=...  47.4 us
    all_to_all x1, waiting for transfers between devices, shards(): lax.all_to_all(lax.all_to_all(w_up, 'cache', split_axis=2, concat_axis=0,...  46.9 us
    all_to_all x1, waiting for transfers between devices, shards(): lax.all_to_all(lax.all_to_all(w_down, 'cache', split_axis=1, concat_axis=...  39.5 us
    all_to_all x1, waiting for transfers between devices, shards(): lax.all_to_all(w_down, 'cache', split_axis=1, concat_axis=0, tiled=True)  23.5 us
    all_to_all x1, waiting for transfers between devices, shards(): lax.all_to_all(w_gate, 'cache', split_axis=2, concat_axis=0, tiled=True)  20 us
    all_gather x3, blocking collectives, joined(): gathered = jax.tree.map(lambda a: lax.all_gather(a, axis), part)  18.5 us
    psum x1, blocking collectives, shards(): expert_out = lax.psum(partial_out, 'cache').astype(jnp.bfloat16)  14.2 us
  transfers between devices with their start and end apart: 8, of which 7 were waited for; matrix products, arithmetic and copies ran while one was open for 16% of the time, Pallas kernels for 0%

profile of v1, /device:TPU:0, one launch (start us, length us, event | category | flops | bytes accessed | tf_op | source)
XLA Modules:
  0.0 366.7 jit_solution(17586536042549778452)
XLA Ops:
  0.7 0.9 add_add_fusion
  2.4 4.0 %copy.74 = bf16[4,1024,256]{1,2,0:T(8,128)(2,1)} copy(bf16[4,1024,256]{2,1,0:T(8,128)(2,1)} %param.14) | data formatting | bytes 4194304 | tf_op args[1]
  6.5 2.1 select_reduce_fusion
  8.6 0.9 copy-done.4
  10.0 6.7 %all_gather.16 = f32[4,2,4,32]{3,2,1,0:T(4,128)} all-gather(f32[1,2,4,32]{3,2,1,0:T(4,128)S(1)} %all_gather_reshape.10), channel_id=1, replica_groups=mesh['cache'=4,'expert'=8] {'cache'}, dimensions={0}, use_global_device_ids=true | all-gather | bytes 5120 | tf_op jit(solution)/shard_map/all_gather | solution.py:20
  17.4 5.8 %all_gather.15 = f32[4,2,4,32]{3,2,1,0:T(4,128)} all-gather(f32[1,2,4,32]{3,2,1,0:T(4,128)S(1)} %all_gather_reshape.9), channel_id=1, replica_groups=mesh['cache'=4,'expert'=8] {'cache'}, dimensions={0}, use_global_device_ids=true | all-gather | bytes 5120 | tf_op jit(solution)/shard_map/all_gather | solution.py:20
  23.9 3.9 %copy.78 = bf16[4,1024,256]{1,2,0:T(8,128)(2,1)} copy(bf16[4,1024,256]{2,1,0:T(8,128)(2,1)} %param.15) | data formatting | bytes 4194304 | tf_op args[2]
  27.9 2.6 convolution_bitcast_fusion.1
  30.6 5.9 %all_gather.17 = f32[4,2,4,2048]{3,2,1,0:T(4,128)S(1)} all-gather(f32[1,2,4,2048]{3,2,1,0:T(4,128)S(1)} %all_gather_reshape.11), channel_id=1, replica_groups=mesh['cache'=4,'expert'=8] {'cache'}, dimensions={0}, use_global_device_ids=true | all-gather | bytes 327680 | tf_op jit(solution)/shard_map/all_gather | solution.py:20
  36.6 3.6 while.19
  41.3 6.6 %all-gather = f32[32,2880]{1,0:T(8,128)S(1)} all-gather(f32[8,2880]{1,0:T(8,128)S(1)} %fusion.39), channel_id=2, replica_groups=mesh['cache'=4,'expert'=8] {'cache'}, dimensions={0}, use_global_device_ids=true | all-gather | bytes 460800 | tf_op jit(solution)/shard_map/all_gather | solution.py:15
  49.5 5.9 %all-to-all-start = ((bf16[8,4,2880]{2,1,0:T(4,128)(2,1)}), bf16[8,4,2880]{2,1,0:T(4,128)(2,1)S(1)}, u32[]{:S(2)}, u32[]{:S(2)}) async-start(bf16[8,4,2880]{2,1,0:T(4,128)(2,1)} %copy.80), calls=%async_computation | async-start | bytes 376832 | tf_op jit(solution)/shard_map/all_to_all | solution.py:132
  55.5 4.6 %copy.81 = bf16[2,360,1440]{1,0,2:T(2,128)(2,1)} copy(bf16[2,360,1440]{2,1,0:T(8,128)(2,1)S(1)} %copy-done.9) | data formatting | bytes 4147200 | tf_op args[6]
  60.1 3.8 %all-to-all-done = bf16[8,4,2880]{2,1,0:T(4,128)(2,1)S(1)} async-done(((bf16[8,4,2880]{2,1,0:T(4,128)(2,1)}), bf16[8,4,2880]{2,1,0:T(4,128)(2,1)S(1)}, u32[]{:S(2)}, u32[]{:S(2)}) %all-to-all-start) | async-done | bytes 184352 | tf_op jit(solution)/shard_map/all_to_all | solution.py:132
  63.8 3.6 all-to-all-start.1
  67.5 6.9 %copy.84 = bf16[2,360,1440]{1,0,2:T(2,128)(2,1)} copy(bf16[2,360,1440]{2,1,0:T(8,128)(2,1)} %param.20) | data formatting | bytes 4147200 | tf_op args[7]
  74.3 20.0 %all-to-all-done.1 = bf16[2,360,1440]{1,0,2:T(2,128)(2,1)S(1)} async-done(((bf16[2,360,1440]{1,0,2:T(2,128)(2,1)}), bf16[2,360,1440]{1,0,2:T(2,128)(2,1)S(1)}, u32[]{:S(2)}, u32[]{:S(2)}) %all-to-all-start.1) | async-done | bytes 2073632 | tf_op jit(solution)/shard_map/all_to_all | solution.py:58
  94.3 1.3 copy-done.8
  95.7 3.6 all-to-all-start.3
  99.3 12.9 %copy.87 = bf16[2,1440,360]{2,0,1:T(2,128)(2,1)} copy(bf16[2,1440,360]{2,1,0:T(8,128)(2,1)} %param.21) | data formatting | bytes 4147200 | tf_op args[8]
  112.2 13.9 %all-to-all-done.3 = bf16[2,360,1440]{1,0,2:T(2,128)(2,1)S(1)} async-done(((bf16[2,360,1440]{1,0,2:T(2,128)(2,1)}), bf16[2,360,1440]{1,0,2:T(2,128)(2,1)S(1)}, u32[]{:S(2)}, u32[]{:S(2)}) %all-to-all-start.3) | async-done | bytes 2073632 | tf_op jit(solution)/shard_map/all_to_all | solution.py:65
  126.1 1.4 copy-done.7
  127.6 3.6 all-to-all-start.5
  131.2 3.3 copy.82
  134.5 23.5 %all-to-all-done.5 = bf16[2,1440,360]{2,0,1:T(2,128)(2,1)S(1)} async-done(((bf16[2,1440,360]{2,0,1:T(2,128)(2,1)}), bf16[2,1440,360]{2,0,1:T(2,128)(2,1)S(1)}, u32[]{:S(2)}, u32[]{:S(2)}) %all-to-all-start.5) | async-done | bytes 2073632 | tf_op jit(solution)/shard_map/all_to_all | solution.py:73
  158.0 1.4 copy-done.6
  159.4 3.6 all-to-all-start.2
  163.0 3.2 copy.85
  166.3 47.4 %all-to-all-done.2 = bf16[8,360,360]{1,2,0:T(8,128)(2,1)S(1)} async-done(((bf16[8,360,360]{1,2,0:T(8,128)(2,1)}), bf16[8,360,360]{1,2,0:T(8,128)(2,1)S(1)}, u32[]{:S(2)}, u32[]{:S(2)}) %all-to-all-start.2) | async-done | bytes 2073632 | tf_op jit(solution)/shard_map/all_to_all | solution.py:57
  213.6 1.4 copy-done.5
  215.0 4.4 %all-to-all-start.4 = ((bf16[8,360,360]{1,2,0:T(8,128)(2,1)}), bf16[8,360,360]{1,2,0:T(8,128)(2,1)}, u32[]{:S(2)}, u32[]{:S(2)}) async-start(bf16[8,360,360]{1,2,0:T(8,128)(2,1)} %bitcast.114), calls=%async_computation.4 | async-start | bytes 4423680 | tf_op jit(solution)/shard_map/all_to_all | solution.py:64
  219.4 3.3 copy.88
  222.7 46.9 %all-to-all-done.4 = bf16[8,360,360]{1,2,0:T(8,128)(2,1)} async-done(((bf16[8,360,360]{1,2,0:T(8,128)(2,1)}), bf16[8,360,360]{1,2,0:T(8,128)(2,1)}, u32[]{:S(2)}, u32[]{:S(2)}) %all-to-all-start.4) | async-done | bytes 2073632 | tf_op jit(solution)/shard_map/all_to_all | solution.py:64
  269.6 3.8 %all-to-all-start.6 = ((bf16[8,360,360]{2,1,0:T(8,128)(2,1)}), bf16[8,360,360]{2,1,0:T(8,128)(2,1)S(1)}, u32[]{:S(2)}, u32[]{:S(2)}) async-start(bf16[8,360,360]{2,1,0:T(8,128)(2,1)} %bitcast.112), calls=%async_computation.6 | async-start | bytes 4423680 | tf_op jit(solution)/shard_map/all_to_all | solution.py:72
  273.5 4.2 %copy.83 = bf16[8,360,360]{2,1,0:T(8,128)(2,1)} copy(bf16[8,360,360]{1,2,0:T(8,128)(2,1)} %copy-done.5) | data formatting | bytes 4147200 | tf_op jit(solution)/shard_map/all_to_all | solution.py:57
  277.7 4.2 %copy.86 = bf16[8,360,360]{2,1,0:T(8,128)(2,1)} copy(bf16[8,360,360]{1,2,0:T(8,128)(2,1)} %all-to-all-done.4) | data formatting | bytes 4147200 | tf_op jit(solution)/shard_map/all_to_all | solution.py:64
  281.9 2.2 fusion.40
  284.7 39.5 %all-to-all-done.6 = bf16[8,360,360]{2,1,0:T(8,128)(2,1)S(1)} async-done(((bf16[8,360,360]{2,1,0:T(8,128)(2,1)}), bf16[8,360,360]{2,1,0:T(8,128)(2,1)S(1)}, u32[]{:S(2)}, u32[]{:S(2)}) %all-to-all-start.6) | async-done | bytes 2073632 | tf_op jit(solution)/shard_map/all_to_all | solution.py:72
  324.2 1.7 copy.89
  325.9 4.8 %reshape.139 = bf16[360,2880,1]{1,0,2:T(8,128)(2,1)} reshape(bf16[1,360,8,360]{3,2,1,0:T(8,128)(2,1)} %copy.89) | data formatting | bytes 4147200 | tf_op jit(solution)/shard_map/squeeze | solution.py:139
  330.7 2.0 fusion.18
  332.7 14.2 %all-reduce.1 = bf16[8,4,2880]{2,0,1:T(8,128)(2,1)S(1)} all-reduce(f32[8,4,2880]{2,0,1:T(8,128)S(1)} %fusion.18), channel_id=1, replica_groups=mesh['cache'=4,'expert'=8] {'cache'}, use_global_device_ids=true, to_apply=%region_8.9 | all-reduce | flops 92160 | bytes 552960 | tf_op jit(solution)/shard_map/psum | solution.py:142
  347.7 4.4 %all-to-all-start.7 = ((bf16[8,4,2880]{2,1,0:T(4,128)(2,1)}), bf16[8,4,2880]{2,1,0:T(4,128)(2,1)S(1)}, u32[]{:S(2)}, u32[]{:S(2)}) async-start(bf16[8,4,2880]{2,1,0:T(4,128)(2,1)} %copy.91), calls=%async_computation.7 | async-start | bytes 376832 | tf_op jit(solution)/shard_map/all_to_all | solution.py:143
  352.1 2.7 copy.95
  354.8 4.3 %copy.96 = bf16[1,2880,360]{1,2,0:T(8,128)(2,1)} copy(bf16[1,2880,360]{2,1,0:T(8,128)(2,1)} %bitcast.106) | data formatting | bytes 4147200
  359.0 2.5 copy.97
  361.5 4.3 %copy.98 = bf16[1,360,2880]{2,1,0:T(8,128)(2,1)} copy(bf16[1,360,2880]{1,2,0:T(8,128)(2,1)} %bitcast.115) | data formatting | bytes 4147200
  365.8 0.9 fusion.4
  (73 shorter events, 10.5 us)
Async XLA Ops:
  0.6 39.8 %copy-start = (bf16[512,2880]{0,1:T(8,128)(2,1)S(1)}, bf16[512,2880]{0,1:T(8,128)(2,1)}, u32[]{:S(2)}) copy-start(bf16[512,2880]{0,1:T(8,128)(2,1)} %param.17) | copy-start | bytes 8847364
  8.6 1.0 copy-start.4
  40.4 7.9 %copy-start.11 = (f32[2,4,4]{2,1,0:T(4,128)S(1)}, f32[2,4,4]{2,1,0:T(4,128)}, u32[]{:S(2)}) copy-start(f32[2,4,4]{2,1,0:T(4,128)} %param.23) | copy-start | bytes 388
  40.4 7.8 %copy-start.12 = (s32[2,4,4]{2,1,0:T(4,128)S(1)}, s32[2,4,4]{2,1,0:T(4,128)}, u32[]{:S(2)}) copy-start(s32[2,4,4]{2,1,0:T(4,128)} %param.22) | copy-start | bytes 388
  40.4 8.1 %copy-start.10 = (f32[2880]{0:T(1024)S(1)}, f32[2880]{0:T(1024)}, u32[]{:S(2)}) copy-start(f32[2880]{0:T(1024)} %param.18) | copy-start | bytes 34564
  41.3 14.2 %copy-start.9 = (bf16[2,360,1440]{2,1,0:T(8,128)(2,1)S(1)}, bf16[2,360,1440]{2,1,0:T(8,128)(2,1)}, u32[]{:S(2)}) copy-start(bf16[2,360,1440]{2,1,0:T(8,128)(2,1)} %param.19) | copy-start | bytes 6220804
  49.5 14.3 %all-to-all-start = ((bf16[8,4,2880]{2,1,0:T(4,128)(2,1)}), bf16[8,4,2880]{2,1,0:T(4,128)(2,1)S(1)}, u32[]{:S(2)}, u32[]{:S(2)}) async-start(bf16[8,4,2880]{2,1,0:T(4,128)(2,1)} %copy.80), calls=%async_computation | async-start | bytes 376832 | tf_op jit(solution)/shard_map/all_to_all | solution.py:132
  63.8 30.5 %all-to-all-start.1 = ((bf16[2,360,1440]{1,0,2:T(2,128)(2,1)}), bf16[2,360,1440]{1,0,2:T(2,128)(2,1)S(1)}, u32[]{:S(2)}, u32[]{:S(2)}) async-start(bf16[2,360,1440]{1,0,2:T(2,128)(2,1)} %copy.81), calls=%async_computation.1 | async-start | bytes 4423680 | tf_op jit(solution)/shard_map/all_to_all | solution.py:58
  94.3 1.3 copy-start.8
  95.7 30.5 %all-to-all-start.3 = ((bf16[2,360,1440]{1,0,2:T(2,128)(2,1)}), bf16[2,360,1440]{1,0,2:T(2,128)(2,1)S(1)}, u32[]{:S(2)}, u32[]{:S(2)}) async-start(bf16[2,360,1440]{1,0,2:T(2,128)(2,1)} %copy.84), calls=%async_computation.3 | async-start | bytes 4423680 | tf_op jit(solution)/shard_map/all_to_all | solution.py:65
  126.1 1.4 copy-start.7
  127.6 30.5 %all-to-all-start.5 = ((bf16[2,1440,360]{2,0,1:T(2,128)(2,1)}), bf16[2,1440,360]{2,0,1:T(2,128)(2,1)S(1)}, u32[]{:S(2)}, u32[]{:S(2)}) async-start(bf16[2,1440,360]{2,0,1:T(2,128)(2,1)} %copy.87), calls=%async_computation.5 | async-start | bytes 4423680 | tf_op jit(solution)/shard_map/all_to_all | solution.py:73
  158.0 1.4 copy-start.6
  159.4 54.2 %all-to-all-start.2 = ((bf16[8,360,360]{1,2,0:T(8,128)(2,1)}), bf16[8,360,360]{1,2,0:T(8,128)(2,1)S(1)}, u32[]{:S(2)}, u32[]{:S(2)}) async-start(bf16[8,360,360]{1,2,0:T(8,128)(2,1)} %bitcast.113), calls=%async_computation.2 | async-start | bytes 4423680 | tf_op jit(solution)/shard_map/all_to_all | solution.py:57
  213.6 1.4 copy-start.5
  215.0 54.6 %all-to-all-start.4 = ((bf16[8,360,360]{1,2,0:T(8,128)(2,1)}), bf16[8,360,360]{1,2,0:T(8,128)(2,1)}, u32[]{:S(2)}, u32[]{:S(2)}) async-start(bf16[8,360,360]{1,2,0:T(8,128)(2,1)} %bitcast.114), calls=%async_computation.4 | async-start | bytes 4423680 | tf_op jit(solution)/shard_map/all_to_all | solution.py:64
  269.6 54.6 %all-to-all-start.6 = ((bf16[8,360,360]{2,1,0:T(8,128)(2,1)}), bf16[8,360,360]{2,1,0:T(8,128)(2,1)S(1)}, u32[]{:S(2)}, u32[]{:S(2)}) async-start(bf16[8,360,360]{2,1,0:T(8,128)(2,1)} %bitcast.112), calls=%async_computation.6 | async-start | bytes 4423680 | tf_op jit(solution)/shard_map/all_to_all | solution.py:72
  281.9 2.3 copy-start.2
  347.7 18.1 %all-to-all-start.7 = ((bf16[8,4,2880]{2,1,0:T(4,128)(2,1)}), bf16[8,4,2880]{2,1,0:T(4,128)(2,1)S(1)}, u32[]{:S(2)}, u32[]{:S(2)}) async-start(bf16[8,4,2880]{2,1,0:T(4,128)(2,1)} %copy.91), calls=%async_computation.7 | async-start | bytes 376832 | tf_op jit(solution)/shard_map/all_to_all | solution.py:143
  354.8 4.3 %copy-start.3 = (bf16[8,360,360]{2,1,0:T(8,128)(2,1)S(1)}, bf16[8,360,360]{2,1,0:T(8,128)(2,1)}, u32[]{:S(2)}) copy-start(bf16[8,360,360]{2,1,0:T(8,128)(2,1)} %copy.86) | copy-start | bytes 6220804
  361.5 5.2 %copy-start.1 = (bf16[512,2880]{0,1:T(8,128)(2,1)S(1)}, bf16[512,2880]{0,1:T(8,128)(2,1)}, u32[]{:S(2)}) copy-start(bf16[512,2880]{0,1:T(8,128)(2,1)} %param.17) | copy-start | bytes 8847364
